TPU v7x, 256 devices: a whole 4x4x8 slice. The times are simulated.
256 devices in a mesh: row: 8 (over z), col: 8 (over y, core), depth: 4 (over x).
Axes of the slice: x: 4, y: 4, z: 8, core: 2. Of those that a mesh axis runs over, the one named last changes fastest.
Arguments:
- a21_leaf: float32 [4, 4096, 2048], P('depth', 'row', 'col'), may hold values from -1.2 to 1.2
- a12_leaf: float32 [4, 2048, 4096], P('depth', 'row', 'col'), may hold values from -1.2 to 1.2
- uinv_leaf: float32 [4, 2048, 2048], P('depth', None, 'col'), may hold values from -0.2 to 1.5, as said below
- linv_leaf: float32 [4, 2048, 2048], P('depth', 'row'), may hold values from -0.2 to 1.5, as said below
- live: int32 [4], P('depth'), may hold values from 16 to 32
- row_map: int32 [4, 32], P('depth', 'row'), may hold values from 0 to 63, as said below
- col_map: int32 [4, 32], P('depth', 'col'), may hold values from 0 to 63, as said below
- a22_anc: float32 [8192, 8192], P(('row', 'depth'), 'col'), may hold values from -6 to 6
- a21_anc: float32 [8192, 2048], P(('row', 'depth'), 'col'), may hold values from -1.2 to 1.2
- a12_anc: float32 [2048, 8192], P(('row', 'depth'), 'col'), may hold values from -1.2 to 1.2
- uinv_anc: float32 [2048, 2048], P(None, 'col'), may hold values from -0.2 to 1.5, as said below
- linv_anc: float32 [2048, 2048], P(('row', 'depth')), may hold values from -0.2 to 1.5, as said below
Outputs:
- leaf_lower: float32 [4, 4096, 2048], P('depth', 'row', 'col')
- leaf_upper: float32 [4, 2048, 4096], P('depth', 'row', 'col')
- anc_lower: float32 [8192, 2048], P(('row', 'depth'), 'col')
- anc_upper: float32 [2048, 8192], P(('row', 'depth'), 'col')
- anc_schur: float32 [8192, 8192], P(('row', 'depth'), 'col')
Inputs may be any that keep to these rules, and one draw needn't show every extreme that they name: `uinv_leaf`: upper triangular: zero below the diagonal, diagonal between 0.5 and 1.5. `linv_leaf`: lower triangular: zero above the diagonal, diagonal between 0.5 and 1.5. `uinv_anc`: upper triangular: zero below the diagonal, diagonal between 0.5 and 1.5. `linv_anc`: lower triangular: zero above the diagonal, diagonal between 0.5 and 1.5. `row_map`: within one replica the entries are distinct. Leaf block row i lies in the k-th of 8 equal ranges of leaf block rows, and its target lies in the k-th of 8 equal ranges of the 64 ancestor block rows. `col_map`: within one replica the entries are distinct. Leaf block column j lies in the k-th of 8 equal ranges of leaf block columns, and its target lies in the k-th of 8 equal ranges of the 64 ancestor block columns.
All inputs are finite; a program needn't handle non-finite values.
Results may differ from a plain program's by a relative error of at most 0.0001.
Values sent between devices are 32-bit elements; how exact they have to be, the bound alone decides.
No kernel may reach another device: no remote copies, remote signals or barrier semaphores. Data moves between devices by JAX's collectives and lax.ppermute only.
A program may use at most 128 MiB of HBM per device.

v0:
```python
import math
import jax
import jax.numpy as jnp
from jax import lax
from jax.sharding import PartitionSpec as P

NB = 128


def in_one_piece(arrays, axis, split_dim, concat_dim, along):
    widths = [math.prod(a.shape[along:]) for a in arrays]
    both = jnp.concatenate(
        [a.reshape(*a.shape[:along], w) for a, w in zip(arrays, widths)], axis=along
    )
    out = lax.all_to_all(both, axis, split_axis=split_dim, concat_axis=concat_dim, tiled=True)
    tiles = jnp.split(out, [sum(widths[:k]) for k in range(1, len(widths))], axis=along)
    return tuple((b.reshape(*out.shape[:along], *a.shape[along:]) for a, b in zip(arrays, tiles)))


def sent_to_all(shard, axis):
    copies = jnp.broadcast_to(shard, (lax.axis_size(axis), *shard.shape))
    return lax.all_to_all(copies, axis, split_axis=0, concat_axis=0, tiled=True)


def in_order(tiles, dim):
    lengths = list(tiles.shape[1:])
    lengths[dim] *= tiles.shape[0]
    return jnp.moveaxis(tiles, 0, dim).reshape(lengths)


def collect(shard, axis, dim):
    tiles = sent_to_all(shard, axis)
    return in_order(tiles, dim)


def gather_axes(shard, axes, dim):
    out = shard
    for number in range(len(axes) - 1, -1, -1):
        out = lax.all_gather(out, axes[number], axis=dim, tiled=True)
    return out


def product(left, right):
    return jnp.dot(left, right, precision=lax.Precision.HIGHEST, preferred_element_type=jnp.float32)


def combine_depth(schur, row_map, col_map, a22_anc):
    block_size = NB
    rows_here = schur.shape[0]
    cols_here = schur.shape[1]
    leaf_rows = rows_here // block_size
    leaf_cols = cols_here // block_size
    anc_rows = a22_anc.shape[0]
    replicas = lax.axis_size("depth")
    anc_row_blocks = anc_rows * replicas // block_size
    anc_col_blocks = a22_anc.shape[1] // block_size
    row_local = row_map[0] - lax.axis_index("row") * anc_row_blocks
    col_local = col_map[0] - lax.axis_index("col") * anc_col_blocks
    owner_blocks = anc_rows // block_size
    slots = min(leaf_rows, owner_blocks)
    owner = row_local // owner_blocks
    earlier = lax.iota(jnp.int32, leaf_rows)[:, None] > lax.iota(jnp.int32, leaf_rows)[None, :]
    same = owner[:, None] == owner[None, :]
    rank = jnp.sum((earlier & same).astype(jnp.int32), axis=1)
    select = (
        (owner[:, None, None] == lax.iota(jnp.int32, replicas)[None, :, None])
        & (rank[:, None, None] == lax.iota(jnp.int32, slots)[None, None, :])
    ).astype(jnp.float32)
    leaf_blocks = schur.reshape(leaf_rows, block_size, cols_here)
    packed = jnp.einsum("iqs,ixc->qsxc", select, leaf_blocks, precision=lax.Precision.HIGHEST)
    packed = packed.reshape(replicas, slots * block_size, cols_here)
    target = (row_local - owner * owner_blocks + 1).astype(jnp.float32)
    tags = jnp.einsum("iqs,i->qs", select, target, precision=lax.Precision.HIGHEST) - 1.0
    col_tags = jnp.broadcast_to(col_local.astype(jnp.float32)[None, :], (replicas, leaf_cols))
    got_rows, got_tags, got_cols = in_one_piece((packed, tags, col_tags), "depth", 0, 0, 1)
    slot_pick = (
        got_tags[:, :, None] == lax.iota(jnp.int32, owner_blocks).astype(jnp.float32)[None, None, :]
    ).astype(jnp.float32)
    column_pick = (
        got_cols[:, :, None]
        == lax.iota(jnp.int32, anc_col_blocks).astype(jnp.float32)[None, None, :]
    ).astype(jnp.float32)
    pieces = got_rows.reshape(replicas, slots, block_size, leaf_cols, block_size)
    sectioned = jnp.einsum("psa,psxjy->paxjy", slot_pick, pieces, precision=lax.Precision.HIGHEST)
    placed = jnp.einsum("paxjy,pjb->axby", sectioned, column_pick, precision=lax.Precision.HIGHEST)
    return placed.reshape(anc_rows, anc_col_blocks * block_size)


def anc_panels(a21_anc, a12_anc, uinv_anc, linv_anc):
    factor = uinv_anc
    anc_lower = product(collect(a21_anc, "col", 1), factor)
    lower_whole = collect(anc_lower, "col", 1)
    factor = linv_anc
    anc_upper = product(factor, lax.all_gather(a12_anc, ("row", "depth"), axis=0, tiled=True))
    return (anc_lower, lower_whole, anc_upper)


def shards(
    a21_leaf,
    a12_leaf,
    uinv_leaf,
    linv_leaf,
    live,
    row_map,
    col_map,
    a22_anc,
    a21_anc,
    a12_anc,
    uinv_anc,
    linv_anc,
):
    block_size = NB
    panel_left = a21_leaf[0]
    panel_top = a12_leaf[0]
    upper_inverse = uinv_leaf[0]
    lower_inverse = linv_leaf[0]
    rows_here = panel_left.shape[0]
    cols_here = panel_top.shape[1]
    live_rows = live[0] * block_size
    row_pos = lax.axis_index("row") * rows_here + lax.iota(jnp.int32, rows_here)
    col_pos = lax.axis_index("col") * cols_here + lax.iota(jnp.int32, cols_here)
    row_keep = (row_pos < live_rows).astype(jnp.float32)
    col_keep = (col_pos < live_rows).astype(jnp.float32)
    factor = upper_inverse
    lower_part = product(lax.all_gather(panel_left, "col", axis=1, tiled=True), factor)
    leaf_lower = lower_part * row_keep[:, None]
    factor = lower_inverse
    upper_part = product(factor, lax.all_gather(panel_top, "row", axis=0, tiled=True))
    leaf_upper = upper_part * col_keep[None, :]
    upper_whole = lax.all_gather(leaf_upper, "row", axis=0, tiled=True)
    factor = upper_whole
    schur = jnp.zeros((rows_here, cols_here), jnp.float32) - product(
        lax.all_gather(leaf_lower, "col", axis=1, tiled=True), factor
    )
    own_update = combine_depth(schur, row_map, col_map, a22_anc)
    anc_lower, lower_whole, anc_upper = anc_panels(a21_anc, a12_anc, uinv_anc, linv_anc)
    factor = lower_whole
    anc_schur = a22_anc + own_update - product(factor, gather_axes(anc_upper, ("row", "depth"), 0))
    return (leaf_lower[None], leaf_upper[None], anc_lower, anc_upper, anc_schur)


def solution(mesh):
    in_specs = (
        P("depth", "row", "col"),
        P("depth", "row", "col"),
        P("depth", None, "col"),
        P("depth", "row", None),
        P("depth"),
        P("depth", "row"),
        P("depth", "col"),
        P(("row", "depth"), "col"),
        P(("row", "depth"), "col"),
        P(("row", "depth"), "col"),
        P(None, "col"),
        P(("row", "depth"), None),
    )
    out_specs = (
        P("depth", "row", "col"),
        P("depth", "row", "col"),
        P(("row", "depth"), "col"),
        P(("row", "depth"), "col"),
        P(("row", "depth"), "col"),
    )
    return jax.shard_map(shards, mesh=mesh, in_specs=in_specs, out_specs=out_specs, check_vma=False)
```

profile of v0, /device:TPU:1, one launch (start us, length us, event | category | flops | bytes accessed | tf_op | source)
XLA Modules:
  0.0 436.7 jit_solution(4254180319421357973)
XLA Ops:
  10.1 38.6 %all-gather.20.cloned.1.call-done = f32[1,512,2048]{2,1,0:T(8,128)} async-done(((f32[1,512,256]{2,1,0:T(8,128)}), f32[1,512,2048]{2,1,0:T(8,128)}) %all-gather.20.cloned.1.call-update) | async-done | bytes 4194320 | tf_op jit(solution)/shard_map/all_gather | solution.py:125
  48.7 6.4 %fusion.10 = f32[512,256]{1,0:T(8,128)} fusion(f32[1,2048,256]{2,1,0:T(8,128)S(1)} %copy-done, f32[1,512,2048]{2,1,0:T(8,128)} %all-gather.20.cloned.1.call-done, f32[512]{0:T(512)S(1)} %fusion.32), kind=kOutput, calls=%fused_computation.13 | convolution fusion | flops 3221356544 | bytes 6817792 | tf_op jit(solution)/shard_map/dot_general | solution.py:44
  55.2 49.4 %all-gather.22.cloned.1.call-done = f32[1,2048,512]{2,1,0:T(8,128)} async-done(((f32[1,256,512]{2,1,0:T(8,128)}), f32[1,2048,512]{2,1,0:T(8,128)}) %all-gather.22.cloned.1.call-update) | async-done | bytes 4194320 | tf_op jit(solution)/shard_map/all_gather | solution.py:128
  104.6 7.3 %fusion.15 = f32[256,512]{1,0:T(8,128)} fusion(f32[1,2048,512]{2,1,0:T(8,128)} %all-gather.22.cloned.1.call-done, f32[1,256,2048]{2,1,0:T(8,128)} %param.15, f32[512]{0:T(512)S(1)} %fusion.33), kind=kOutput, calls=%fused_computation.14 | convolution fusion | flops 3221356544 | bytes 6817792 | tf_op jit(solution)/shard_map/dot_general | solution.py:44
  113.6 5.3 %all-to-all-start = ((f32[8,256,256]{1,2,0:T(8,128)}), f32[8,256,256]{1,2,0:T(8,128)S(1)}, u32[]{:S(2)}, u32[]{:S(2)}) async-start(f32[8,256,256]{1,2,0:T(8,128)} %broadcast_in_dim.16), calls=%async_computation | async-start | bytes 4194304 | tf_op jit(solution)/shard_map/all_to_all | solution.py:22
  119.0 84.1 %all-gather.10.cloned.1.call-done = f32[2048,1024]{1,0:T(8,128)} async-done(((f32[64,1024]{1,0:T(8,128)}), f32[2048,1024]{1,0:T(8,128)}) %all-gather.10.cloned.1.call-update) | async-done | bytes 8388624 | tf_op jit(solution)/shard_map/all_gather | solution.py:94
  203.1 8.2 %fusion.51 = f32[64,1024]{1,0:T(8,128)} fusion(f32[64,2048]{1,0:T(8,128)S(1)} %copy-done.3, f32[2048,1024]{1,0:T(8,128)} %all-gather.10.cloned.1.call-done), kind=kOutput, calls=%fused_computation.69 | convolution fusion | flops 1610612736 | bytes 9175040 | tf_op jit(solution)/shard_map/dot_general | solution.py:44
  211.9 26.4 %all-gather.12.cloned.1.call-done = f32[512,2048]{1,0:T(8,128)} async-done(((f32[512,256]{1,0:T(8,128)}), f32[512,2048]{1,0:T(8,128)}) %all-gather.12.cloned.1.call-update) | async-done | bytes 4194320 | tf_op jit(solution)/shard_map/all_gather | solution.py:133
  238.3 56.4 %all-gather.14.cloned.1.call-done = f32[2048,512]{1,0:T(8,128)} async-done(((f32[256,512]{1,0:T(8,128)}), f32[2048,512]{1,0:T(8,128)}) %all-gather.14.cloned.1.call-update) | async-done | bytes 4194320 | tf_op jit(solution)/shard_map/all_gather | solution.py:130
  294.7 9.4 %convolution_subtract_fusion = f32[512,512]{1,0:T(8,128)S(1)} fusion(f32[512,2048]{1,0:T(8,128)} %all-gather.12.cloned.1.call-done, f32[2048,512]{1,0:T(8,128)} %all-gather.14.cloned.1.call-done), kind=kOutput, calls=%fused_computation.11 | convolution fusion | flops 6442713088 | bytes 9437184 | tf_op jit(solution)/shard_map/dot_general | solution.py:44
  304.0 3.6 fusion.20
  307.6 12.7 %all-gather.16.cloned.1.call-done = f32[256,1024]{1,0:T(8,128)} async-done(((f32[64,1024]{1,0:T(8,128)}), f32[256,1024]{1,0:T(8,128)}) %all-gather.16.cloned.1.call-update) | async-done | bytes 1048592 | tf_op jit(solution)/shard_map/all_gather | solution.py:39
  320.3 3.1 constant_dynamic-update-slice_fusion
  326.0 4.8 %copy.31 = f32[4,1,131078]{2,1,0:T(1,128)} copy(f32[4,1,131078]{2,0,1:T(4,128)} %bitcast.99) | data formatting | bytes 4194496 | tf_op jit(solution)/shard_map/all_to_all | solution.py:15
  330.9 4.5 %all-to-all-start.1 = ((f32[4,1,131078]{2,1,0:T(1,128)}), f32[4,1,131078]{2,1,0:T(1,128)}, u32[]{:S(2)}, u32[]{:S(2)}) async-start(f32[4,1,131078]{2,1,0:T(1,128)} %copy.31), calls=%async_computation.1 | async-start | bytes 4198400 | tf_op jit(solution)/shard_map/all_to_all | solution.py:15
  335.4 5.3 %fusion.50 = f32[256,256]{1,0:T(8,128)S(1)} fusion(f32[256,2048]{0,1:T(8,128)S(1)} %bitcast.100, f32[2048,256]{1,0:T(8,128)} %param.22), kind=kOutput, calls=%fused_computation.68 | convolution fusion | flops 1610612736 | bytes 4456448 | tf_op jit(solution)/shard_map/dot_general | solution.py:44
  340.8 18.3 %all-to-all-done.1 = f32[4,1,131078]{2,1,0:T(1,128)} async-done(((f32[4,1,131078]{2,1,0:T(1,128)}), f32[4,1,131078]{2,1,0:T(1,128)}, u32[]{:S(2)}, u32[]{:S(2)}) %all-to-all-start.1) | async-done | bytes 2097280 | tf_op jit(solution)/shard_map/all_to_all | solution.py:15
  360.6 7.9 %all-to-all-start.2 = ((f32[8,256,256]{1,2,0:T(8,128)}), f32[8,256,256]{1,2,0:T(8,128)}, u32[]{:S(2)}, u32[]{:S(2)}) async-start(f32[8,256,256]{1,2,0:T(8,128)} %broadcast_in_dim.20), calls=%async_computation.2 | async-start | bytes 4194304 | tf_op jit(solution)/shard_map/all_to_all | solution.py:22
  372.8 3.4 reshape_reshape.7
  376.2 4.8 %fusion.8 = f32[4,2,128,4,128]{4,1,3,2,0:T(2,128)S(1)} fusion(f32[4,2,128,4,128]{4,3,2,1,0:T(4,128)S(1)} %reshape_reshape.7, f32[4,2]{1,0:T(4,128)S(1)} %split.13, f32[2]{0:T(128)S(1)} %iota_convert_fusion), kind=kOutput, calls=%fused_computation.9 | convolution fusion | flops 12582928 | bytes 4194344 | tf_op jit(solution)/shard_map/psa,psxjy->paxjy/dot_general | solution.py:84
  381.0 3.2 fusion.6
  384.3 10.6 %all-to-all-done.2 = f32[8,256,256]{1,2,0:T(8,128)} async-done(((f32[8,256,256]{1,2,0:T(8,128)}), f32[8,256,256]{1,2,0:T(8,128)}, u32[]{:S(2)}, u32[]{:S(2)}) %all-to-all-start.2) | async-done | bytes 2097184 | tf_op jit(solution)/shard_map/all_to_all | solution.py:22
  394.8 23.6 %all-gather.18.cloned.1.call-done = f32[2048,1024]{1,0:T(8,128)} async-done(((f32[256,1024]{1,0:T(8,128)}), f32[2048,1024]{1,0:T(8,128)}) %all-gather.18.cloned.1.call-update) | async-done | bytes 8388624 | tf_op jit(solution)/shard_map/all_gather | solution.py:39
  418.5 11.4 %convolution_subtract_fusion.1 = f32[256,1024]{1,0:T(8,128)} fusion(f32[256,2048]{0,1:T(8,128)} %bitcast.28, f32[2048,1024]{1,0:T(8,128)} %all-gather.18.cloned.1.call-done, f32[256,1024]{1,0:T(8,128)} %param.19, f32[32,8,8,128]{3,2,1,0:T(8,128)S(1)} %bitcast.103), kind=kOutput, calls=%fused_computation.12 | convolution fusion | flops 6442975232 | bytes 13631488 | tf_op jit(solution)/shard_map/dot_general | solution.py:44
  (54 shorter events, 13.2 us)
Async XLA Ops:
  7.2 41.5 %copy-start = (f32[1,2048,256]{2,1,0:T(8,128)S(1)}, f32[1,2048,256]{2,1,0:T(8,128)}, u32[]{:S(2)}) copy-start(f32[1,2048,256]{2,1,0:T(8,128)} %param.14) | copy-start | bytes 6291460
  7.2 41.5 %all-gather.20.cloned.1.call-start = ((), (), s32[]{:S(2)}) async-start(), calls=%async_computation.8 | async-start | bytes 4718592 | tf_op jit(solution)/shard_map/all_gather | solution.py:125
  7.9 96.7 %all-gather.22.cloned.1.call-start = ((), (), s32[]{:S(2)}) async-start(), calls=%async_computation.9 | async-start | bytes 4718592 | tf_op jit(solution)/shard_map/all_gather | solution.py:128
  8.7 194.5 %all-gather.10.cloned.1.call-start = ((), (), s32[]{:S(2)}) async-start(), calls=%async_computation.3 | async-start | bytes 8650752 | tf_op jit(solution)/shard_map/all_gather | solution.py:94
  9.4 228.9 %all-gather.12.cloned.1.call-start = ((), (), s32[]{:S(2)}) async-start(), calls=%async_computation.4 | async-start | bytes 4718592 | tf_op jit(solution)/shard_map/all_gather | solution.py:133
  55.1 239.5 %all-gather.14.cloned.1.call-start = ((), (), s32[]{:S(2)}) async-start(), calls=%async_computation.5 | async-start | bytes 4718592 | tf_op jit(solution)/shard_map/all_gather | solution.py:130
  55.2 56.8 %copy-start.4 = (f32[256,256]{1,0:T(8,128)S(1)}, f32[256,256]{1,0:T(8,128)}, u32[]{:S(2)}) copy-start(f32[256,256]{1,0:T(8,128)} %param.20) | copy-start | bytes 786436
  113.6 5.3 %copy-start.5 = (s32[1,4]{1,0:T(1,128)S(1)}, s32[1,4]{1,0:T(1,128)}, u32[]{:S(2)}) copy-start(s32[1,4]{1,0:T(1,128)} %param.17) | copy-start | bytes 52
  113.6 89.5 %copy-start.3 = (f32[64,2048]{1,0:T(8,128)S(1)}, f32[64,2048]{1,0:T(8,128)}, u32[]{:S(2)}) copy-start(f32[64,2048]{1,0:T(8,128)} %param.23) | copy-start | bytes 1572868
  113.6 217.2 %all-to-all-start = ((f32[8,256,256]{1,2,0:T(8,128)}), f32[8,256,256]{1,2,0:T(8,128)S(1)}, u32[]{:S(2)}, u32[]{:S(2)}) async-start(f32[8,256,256]{1,2,0:T(8,128)} %broadcast_in_dim.16), calls=%async_computation | async-start | bytes 4194304 | tf_op jit(solution)/shard_map/all_to_all | solution.py:22
  118.9 201.4 %all-gather.16.cloned.1.call-start = ((), (), s32[]{:S(2)}) async-start(), calls=%async_computation.6 | async-start | bytes 1310720 | tf_op jit(solution)/shard_map/all_gather | solution.py:39
  119.0 92.8 %copy-start.6 = (s32[1,4]{1,0:T(1,128)S(1)}, s32[1,4]{1,0:T(1,128)}, u32[]{:S(2)}) copy-start(s32[1,4]{1,0:T(1,128)} %param.18) | copy-start | bytes 52
  211.4 207.1 %all-gather.18.cloned.1.call-start = ((), (), s32[]{:S(2)}) async-start(), calls=%async_computation.7 | async-start | bytes 9437184 | tf_op jit(solution)/shard_map/all_gather | solution.py:39
  330.9 28.3 %all-to-all-start.1 = ((f32[4,1,131078]{2,1,0:T(1,128)}), f32[4,1,131078]{2,1,0:T(1,128)}, u32[]{:S(2)}, u32[]{:S(2)}) async-start(f32[4,1,131078]{2,1,0:T(1,128)} %copy.31), calls=%async_computation.1 | async-start | bytes 4198400 | tf_op jit(solution)/shard_map/all_to_all | solution.py:15
  340.7 20.0 %copy-start.2 = (f32[256,256]{1,0:T(8,128)}, f32[256,256]{1,0:T(8,128)S(1)}, u32[]{:S(2)}) copy-start(f32[256,256]{1,0:T(8,128)S(1)} %fusion.50) | copy-start | bytes 786436
  360.6 34.2 %all-to-all-start.2 = ((f32[8,256,256]{1,2,0:T(8,128)}), f32[8,256,256]{1,2,0:T(8,128)}, u32[]{:S(2)}, u32[]{:S(2)}) async-start(f32[8,256,256]{1,2,0:T(8,128)} %broadcast_in_dim.20), calls=%async_computation.2 | async-start | bytes 4194304 | tf_op jit(solution)/shard_map/all_to_all | solution.py:22
  418.5 11.4 %copy-start.1 = (f32[1,2048,256]{2,1,0:T(8,128)S(1)}, f32[1,2048,256]{2,1,0:T(8,128)}, u32[]{:S(2)}) copy-start(f32[1,2048,256]{2,1,0:T(8,128)} %param.14) | copy-start | bytes 6291460
Sparse Core Ops, SparseCore 0:
  9.8 38.8 all-gather.19
  50.5 54.1 all-gather.21
  107.2 95.8 all-gather.9
  205.4 32.8 all-gather.11
  240.5 54.1 all-gather.13
  296.9 23.3 all-gather.15
  322.0 96.3 all-gather.17
where the time goes:
time: 437 us
  waiting for transfers between devices  322 us (74%)
  matrix products  59.7 us (14%)
  local copies, waits for them, and re-layouts  21.7 us (5%)
  starting transfers between devices  18.1 us (4%)
  between operations  14.9 us (3%)
    all_gather x1, waiting for transfers between devices, anc_panels(): lax.all_gather(a12_anc, ('row', 'depth'), axis=0, tiled=True)  84.1 us
    all_gather x1, waiting for transfers between devices, shards(): upper_whole = lax.all_gather(leaf_upper, 'row', axis=0, tiled=True)  56.4 us
    all_gather x1, waiting for transfers between devices, shards(): lax.all_gather(panel_top, 'row', axis=0, tiled=True)  49.4 us
    dot_general x6, matrix products, product(): jnp.dot(left, right, precision=lax.Precision.HIGHEST, preferred_element_t...  48 us
    all_gather x1, waiting for transfers between devices, shards(): lax.all_gather(panel_left, 'col', axis=1, tiled=True)  38.6 us
    all_gather x2, waiting for transfers between devices, gather_axes(): out = lax.all_gather(out, axes[number], axis=dim, tiled=True)  36.3 us
    all_gather x1, waiting for transfers between devices, shards(): lax.all_gather(leaf_lower, 'col', axis=1, tiled=True)  26.4 us
    all_to_all x1, waiting for transfers between devices, in_one_piece(): lax.all_to_all(both, axis, split_axis=split_dim, concat_axis=concat_dim,...  18.3 us
  transfers between devices with their start and end apart: 10, of which 9 were waited for; matrix products, arithmetic and copies ran while one was open for 16% of the time, Pallas kernels for 0%

commit v1 on v0

--- a/solution.py
+++ b/solution.py
@@ -5,6 +5,27 @@
 from jax.sharding import PartitionSpec as P
 
 NB = 128
+
+
+def ring_gather(x, axis, dim):
+    size, here, extent = (lax.axis_size(axis), lax.axis_index(axis), x.shape[dim])
+    upward = [(i, (i + 1) % size) for i in range(size)]
+    behind = [(i, (i - 1) % size) for i in range(size)]
+    out = jnp.zeros((*x.shape[:dim], size * extent, *x.shape[dim + 1 :]), x.dtype)
+    out = lax.dynamic_update_slice_in_dim(out, x, here * extent, axis=dim)
+    from_left = from_right = x
+    halfway = size // 2
+    for step in range(1, halfway + 1):
+        from_left = lax.ppermute(from_left, axis, upward)
+        out = lax.dynamic_update_slice_in_dim(
+            out, from_left, (here - step) % size * extent, axis=dim
+        )
+        if step < size - halfway:
+            from_right = lax.ppermute(from_right, axis, behind)
+            out = lax.dynamic_update_slice_in_dim(
+                out, from_right, (here + step) % size * extent, axis=dim
+            )
+    return out
 
 
 def in_one_piece(arrays, axis, split_dim, concat_dim, along):
@@ -125,7 +146,7 @@
     lower_part = product(lax.all_gather(panel_left, "col", axis=1, tiled=True), factor)
     leaf_lower = lower_part * row_keep[:, None]
     factor = lower_inverse
-    upper_part = product(factor, lax.all_gather(panel_top, "row", axis=0, tiled=True))
+    upper_part = product(factor, ring_gather(panel_top, "row", 0))
     leaf_upper = upper_part * col_keep[None, :]
     upper_whole = lax.all_gather(leaf_upper, "row", axis=0, tiled=True)
     factor = upper_whole

time: 437 us -> 387 us (0.89); the launches traced: 437 us -> 382 us
  waiting for transfers between devices: 322 us -> 244 us
  starting transfers between devices: 18.1 us -> 34.3 us
  local copies, waits for them, and re-layouts: 21.7 us -> 27.5 us
    all_gather x1 -> x0, waiting for transfers between devices: 49.4 us -> none  [shards(): lax.all_gather(panel_top, 'row', axis=0, tiled=True)]
    ppermute x0 -> x7, waiting for transfers between devices: none -> 40 us  [the longest x4 40 us: ring_gather(): from_left = lax.ppermute(from_left, axis, upward)]
    all_gather x1, waiting for transfers between devices: 38.6 us -> 0.02 us  [shards(): lax.all_gather(panel_left, 'col', axis=1, tiled=True)]
    all_gather x1, waiting for transfers between devices: 84.1 us -> 55.4 us  [anc_panels(): lax.all_gather(a12_anc, ('row', 'depth'), axis=0, tiled=True)]
    ppermute x0 -> x7, starting transfers between devices: none -> 11.7 us  [the longest x3 8.67 us: ring_gather(): from_right = lax.ppermute(from_right, axis, behind)]
    all_gather x1, waiting for transfers between devices: 56.4 us -> 46.2 us  [shards(): upper_whole = lax.all_gather(leaf_upper, 'row', axis=0, tiled=True)]
    all_gather x1, waiting for transfers between devices: 26.4 us -> 36.1 us  [shards(): lax.all_gather(leaf_lower, 'col', axis=1, tiled=True)]
    unnamed x18 -> x27, local copies, waits for them, and re-layouts: 7.18 us -> 8.96 us
  transfers between devices with their start and end apart: 10 -> 16, of which waited for: 9 -> 11; matrix products, arithmetic and copies ran while one was open for 16% -> 20% of each run, Pallas kernels for 0% -> 0%
where the time goes in v1:
time: 387 us; the launch traced here: 382 us
  waiting for transfers between devices  244 us (63%)
  matrix products  61 us (16%)
  starting transfers between devices  34.3 us (9%)
  local copies, waits for them, and re-layouts  27.5 us (7%)
  between operations  15.4 us (4%)
    all_gather x1, waiting for transfers between devices, anc_panels(): lax.all_gather(a12_anc, ('row', 'depth'), axis=0, tiled=True)  55.4 us
    dot_general x6, matrix products, product(): jnp.dot(left, right, precision=lax.Precision.HIGHEST, preferred_element_t...  49.3 us
    all_gather x1, waiting for transfers between devices, shards(): upper_whole = lax.all_gather(leaf_upper, 'row', axis=0, tiled=True)  46.2 us
    ppermute x4, waiting for transfers between devices, ring_gather(): from_left = lax.ppermute(from_left, axis, upward)  40 us
    all_gather x2, waiting for transfers between devices, gather_axes(): out = lax.all_gather(out, axes[number], axis=dim, tiled=True)  36.7 us
    all_gather x1, waiting for transfers between devices, shards(): lax.all_gather(leaf_lower, 'col', axis=1, tiled=True)  36.1 us
    all_to_all x1, waiting for transfers between devices, in_one_piece(): lax.all_to_all(both, axis, split_axis=split_dim, concat_axis=concat_dim,...  18.3 us
    all_to_all x2, starting transfers between devices, sent_to_all(): return lax.all_to_all(copies, axis, split_axis=0, concat_axis=0, tiled=True)  17.5 us
  transfers between devices with their start and end apart: 16, of which 11 were waited for; matrix products, arithmetic and copies ran while one was open for 20% of the time, Pallas kernels for 0%

profile of v1, /device:TPU:1, one launch (start us, length us, event | category | flops | bytes accessed | tf_op | source)
XLA Modules:
  0.0 382.1 jit_solution(6569275727245892543)
XLA Ops:
  11.3 4.0 %collective-permute-start.1 = (f32[256,512]{1,0:T(8,128)}, f32[256,512]{1,0:T(8,128)S(1)}, u32[]{:S(2)}, u32[]{:S(2)}) collective-permute-start(f32[256,512]{1,0:T(8,128)} %bitcast.108), channel_id=1, source_target_pairs={{0,224},{32,0},{64,32},{96,64},{128,96},{160,128},{192,160},{224,1... | collective-permute-start | bytes 1572872 | tf_op jit(solution)/shard_map/ppermute | solution.py:24
  15.3 11.7 %collective-permute-done = f32[256,512]{1,0:T(8,128)S(1)} collective-permute-done((f32[256,512]{1,0:T(8,128)}, f32[256,512]{1,0:T(8,128)S(1)}, u32[]{:S(2)}, u32[]{:S(2)}) %collective-permute-start) | collective-permute-done | bytes 524320 | tf_op jit(solution)/shard_map/ppermute | solution.py:19
  29.7 10.9 %collective-permute-done.2 = f32[256,512]{1,0:T(8,128)} collective-permute-done((f32[256,512]{1,0:T(8,128)S(1)}, f32[256,512]{1,0:T(8,128)}, u32[]{:S(2)}, u32[]{:S(2)}) %collective-permute-start.2) | collective-permute-done | bytes 524320 | tf_op jit(solution)/shard_map/ppermute | solution.py:19
  44.7 8.8 %collective-permute-done.4 = f32[256,512]{1,0:T(8,128)} collective-permute-done((f32[256,512]{1,0:T(8,128)}, f32[256,512]{1,0:T(8,128)}, u32[]{:S(2)}, u32[]{:S(2)}) %collective-permute-start.4) | collective-permute-done | bytes 524320 | tf_op jit(solution)/shard_map/ppermute | solution.py:19
  57.4 8.6 %collective-permute-done.6 = f32[256,512]{1,0:T(8,128)S(1)} collective-permute-done((f32[256,512]{1,0:T(8,128)}, f32[256,512]{1,0:T(8,128)S(1)}, u32[]{:S(2)}, u32[]{:S(2)}) %collective-permute-start.6) | collective-permute-done | bytes 524320 | tf_op jit(solution)/shard_map/ppermute | solution.py:19
  66.0 7.6 %fusion.9 = f32[512,256]{1,0:T(8,128)} fusion(f32[2048,512]{1,0:T(8,128)S(1)} %constant_dynamic-update-slice_fusion.1, f32[1,256,2048]{2,1,0:T(8,128)S(1)} %copy-done, f32[512]{0:T(512)S(1)} %fusion.30), kind=kOutput, calls=%fused_computation.12 | convolution fusion | flops 3221356544 | bytes 6817792 | tf_op jit(solution)/shard_map/dot_general | solution.py:65
  73.7 7.2 %fusion.12 = f32[512,256]{1,0:T(8,128)} fusion(f32[1,2048,256]{2,1,0:T(8,128)} %param.14, f32[1,512,2048]{2,1,0:T(8,128)} %all-gather.18.cloned.1.call-done, f32[512]{0:T(512)S(1)} %fusion.29), kind=kOutput, calls=%fused_computation.13 | convolution fusion | flops 3221356544 | bytes 6817792 | tf_op jit(solution)/shard_map/dot_general | solution.py:65
  82.6 9.6 %all-to-all-start = ((f32[8,256,256]{1,2,0:T(8,128)}), f32[8,256,256]{1,2,0:T(8,128)S(1)}, u32[]{:S(2)}, u32[]{:S(2)}) async-start(f32[8,256,256]{1,2,0:T(8,128)} %broadcast_in_dim.19), calls=%async_computation | async-start | bytes 4194304 | tf_op jit(solution)/shard_map/all_to_all | solution.py:43
  92.6 55.4 %all-gather.8.cloned.1.call-done = f32[2048,1024]{1,0:T(8,128)} async-done(((f32[64,1024]{1,0:T(8,128)}), f32[2048,1024]{1,0:T(8,128)}) %all-gather.8.cloned.1.call-update) | async-done | bytes 8388624 | tf_op jit(solution)/shard_map/all_gather | solution.py:115
  148.0 8.2 %fusion.48 = f32[64,1024]{1,0:T(8,128)} fusion(f32[64,2048]{1,0:T(8,128)S(1)} %copy-done.4, f32[2048,1024]{1,0:T(8,128)} %all-gather.8.cloned.1.call-done), kind=kOutput, calls=%fused_computation.76 | convolution fusion | flops 1610612736 | bytes 9175040 | tf_op jit(solution)/shard_map/dot_general | solution.py:65
  156.6 46.2 %all-gather.12.cloned.1.call-done = f32[2048,512]{0,1:T(8,128)} async-done(((f32[256,512]{0,1:T(8,128)}), f32[2048,512]{0,1:T(8,128)}) %all-gather.12.cloned.1.call-update) | async-done | bytes 4194320 | tf_op jit(solution)/shard_map/all_gather | solution.py:151
  202.8 36.1 %all-gather.10.cloned.1.call-done = f32[512,2048]{1,0:T(8,128)} async-done(((f32[512,256]{1,0:T(8,128)}), f32[512,2048]{1,0:T(8,128)}) %all-gather.10.cloned.1.call-update) | async-done | bytes 4194320 | tf_op jit(solution)/shard_map/all_gather | solution.py:154
  238.9 9.4 %convolution_subtract_fusion = f32[512,512]{1,0:T(8,128)S(1)} fusion(f32[512,2048]{1,0:T(8,128)} %all-gather.10.cloned.1.call-done, f32[2048,512]{0,1:T(8,128)} %all-gather.12.cloned.1.call-done), kind=kOutput, calls=%fused_computation.10 | convolution fusion | flops 6442713088 | bytes 9437184 | tf_op jit(solution)/shard_map/dot_general | solution.py:65
  248.3 3.6 fusion.17
  251.9 13.4 %all-gather.14.cloned.1.call-done = f32[256,1024]{1,0:T(8,128)} async-done(((f32[64,1024]{1,0:T(8,128)}), f32[256,1024]{1,0:T(8,128)}) %all-gather.14.cloned.1.call-update) | async-done | bytes 1048592 | tf_op jit(solution)/shard_map/all_gather | solution.py:60
  271.1 4.8 %copy.34 = f32[4,1,131078]{2,1,0:T(1,128)} copy(f32[4,1,131078]{2,0,1:T(4,128)} %bitcast.99) | data formatting | bytes 4194496 | tf_op jit(solution)/shard_map/all_to_all | solution.py:36
  275.9 4.7 %all-to-all-start.1 = ((f32[4,1,131078]{2,1,0:T(1,128)}), f32[4,1,131078]{2,1,0:T(1,128)}, u32[]{:S(2)}, u32[]{:S(2)}) async-start(f32[4,1,131078]{2,1,0:T(1,128)} %copy.34), calls=%async_computation.1 | async-start | bytes 4198400 | tf_op jit(solution)/shard_map/all_to_all | solution.py:36
  280.6 5.3 %fusion.47 = f32[256,256]{1,0:T(8,128)S(1)} fusion(f32[256,2048]{0,1:T(8,128)S(1)} %bitcast.100, f32[2048,256]{1,0:T(8,128)} %param.22), kind=kOutput, calls=%fused_computation.75 | convolution fusion | flops 1610612736 | bytes 4456448 | tf_op jit(solution)/shard_map/dot_general | solution.py:65
  286.0 18.3 %all-to-all-done.1 = f32[4,1,131078]{2,1,0:T(1,128)} async-done(((f32[4,1,131078]{2,1,0:T(1,128)}), f32[4,1,131078]{2,1,0:T(1,128)}, u32[]{:S(2)}, u32[]{:S(2)}) %all-to-all-start.1) | async-done | bytes 2097280 | tf_op jit(solution)/shard_map/all_to_all | solution.py:36
  305.8 7.9 %all-to-all-start.2 = ((f32[8,256,256]{1,2,0:T(8,128)}), f32[8,256,256]{1,2,0:T(8,128)}, u32[]{:S(2)}, u32[]{:S(2)}) async-start(f32[8,256,256]{1,2,0:T(8,128)} %broadcast_in_dim.23), calls=%async_computation.2 | async-start | bytes 4194304 | tf_op jit(solution)/shard_map/all_to_all | solution.py:43
  322.5 4.8 %fusion.7 = f32[4,2,128,4,128]{4,1,3,2,0:T(2,128)S(1)} fusion(f32[4,2,128,4,128]{4,3,2,1,0:T(4,128)S(1)} %reshape_reshape.7, f32[4,2]{1,0:T(4,128)S(1)} %split.13, f32[2]{0:T(128)S(1)} %iota_convert_fusion), kind=kOutput, calls=%fused_computation.8 | convolution fusion | flops 12582928 | bytes 4194344 | tf_op jit(solution)/shard_map/psa,psxjy->paxjy/dot_general | solution.py:105
  330.5 9.6 %all-to-all-done.2 = f32[8,256,256]{1,2,0:T(8,128)} async-done(((f32[8,256,256]{1,2,0:T(8,128)}), f32[8,256,256]{1,2,0:T(8,128)}, u32[]{:S(2)}, u32[]{:S(2)}) %all-to-all-start.2) | async-done | bytes 2097184 | tf_op jit(solution)/shard_map/all_to_all | solution.py:43
  340.0 23.3 %all-gather.16.cloned.1.call-done = f32[2048,1024]{1,0:T(8,128)} async-done(((f32[256,1024]{1,0:T(8,128)}), f32[2048,1024]{1,0:T(8,128)}) %all-gather.16.cloned.1.call-update) | async-done | bytes 8388624 | tf_op jit(solution)/shard_map/all_gather | solution.py:60
  363.3 11.7 %convolution_subtract_fusion.1 = f32[256,1024]{1,0:T(8,128)} fusion(f32[256,2048]{0,1:T(8,128)} %bitcast.29, f32[2048,1024]{1,0:T(8,128)} %all-gather.16.cloned.1.call-done, f32[256,1024]{1,0:T(8,128)} %param.19, f32[32,8,8,128]{3,2,1,0:T(8,128)S(1)} %bitcast.105), kind=kOutput, calls=%fused_computation.11 | convolution fusion | flops 6442975232 | bytes 13631488 | tf_op jit(solution)/shard_map/dot_general | solution.py:65
  (83 shorter events, 35.7 us)
Async XLA Ops:
  7.2 58.8 %copy-start = (f32[1,256,2048]{2,1,0:T(8,128)S(1)}, f32[1,256,2048]{2,1,0:T(8,128)}, u32[]{:S(2)}) copy-start(f32[1,256,2048]{2,1,0:T(8,128)} %param.15) | copy-start | bytes 6291460
  7.2 34.6 %copy-start.5 = (f32[1,256,512]{2,1,0:T(8,128)S(1)}, f32[1,256,512]{2,1,0:T(8,128)}, u32[]{:S(2)}) copy-start(f32[1,256,512]{2,1,0:T(8,128)} %param.13) | copy-start | bytes 1572868
  7.2 66.5 %all-gather.18.cloned.1.call-start = ((), (), s32[]{:S(2)}) async-start(), calls=%async_computation.8 | async-start | bytes 4718592 | tf_op jit(solution)/shard_map/all_gather | solution.py:146
  7.9 140.1 %all-gather.8.cloned.1.call-start = ((), (), s32[]{:S(2)}) async-start(), calls=%async_computation.3 | async-start | bytes 8650752 | tf_op jit(solution)/shard_map/all_gather | solution.py:115
  8.7 194.1 %all-gather.12.cloned.1.call-start = ((), (), s32[]{:S(2)}) async-start(), calls=%async_computation.5 | async-start | bytes 4718592 | tf_op jit(solution)/shard_map/all_gather | solution.py:151
  8.7 18.3 %collective-permute-start = (f32[256,512]{1,0:T(8,128)}, f32[256,512]{1,0:T(8,128)S(1)}, u32[]{:S(2)}, u32[]{:S(2)}) collective-permute-start(f32[256,512]{1,0:T(8,128)} %bitcast.107), channel_id=1, source_target_pairs={{0,32},{32,64},{64,96},{96,128},{128,160},{160,192},{192,224},{224... | collective-permute-start | bytes 1572872 | tf_op jit(solution)/shard_map/ppermute | solution.py:19
  11.3 15.8 %collective-permute-start.1 = (f32[256,512]{1,0:T(8,128)}, f32[256,512]{1,0:T(8,128)S(1)}, u32[]{:S(2)}, u32[]{:S(2)}) collective-permute-start(f32[256,512]{1,0:T(8,128)} %bitcast.108), channel_id=1, source_target_pairs={{0,224},{32,0},{64,32},{96,64},{128,96},{160,128},{192,160},{224,1... | collective-permute-start | bytes 1572872 | tf_op jit(solution)/shard_map/ppermute | solution.py:24
  27.0 13.5 %collective-permute-start.2 = (f32[256,512]{1,0:T(8,128)S(1)}, f32[256,512]{1,0:T(8,128)}, u32[]{:S(2)}, u32[]{:S(2)}) collective-permute-start(f32[256,512]{1,0:T(8,128)S(1)} %collective-permute-done), channel_id=1, source_target_pairs={{0,32},{32,64},{64,96},{96,128},{128,160},{160,192},{192,224},{224... | collective-permute-start | bytes 1572872 | tf_op jit(solution)/shard_map/ppermute | solution.py:19
  27.8 14.1 %collective-permute-start.3 = (f32[256,512]{1,0:T(8,128)S(1)}, f32[256,512]{1,0:T(8,128)}, u32[]{:S(2)}, u32[]{:S(2)}) collective-permute-start(f32[256,512]{1,0:T(8,128)S(1)} %collective-permute-done.1), channel_id=1, source_target_pairs={{0,224},{32,0},{64,32},{96,64},{128,96},{160,128},{192,160},{224,1... | collective-permute-start | bytes 1572872 | tf_op jit(solution)/shard_map/ppermute | solution.py:24
  40.6 12.9 %collective-permute-start.4 = (f32[256,512]{1,0:T(8,128)}, f32[256,512]{1,0:T(8,128)}, u32[]{:S(2)}, u32[]{:S(2)}) collective-permute-start(f32[256,512]{1,0:T(8,128)} %collective-permute-done.2), channel_id=1, source_target_pairs={{0,32},{32,64},{64,96},{96,128},{128,160},{160,192},{192,224},{224... | collective-permute-start | bytes 1572872 | tf_op jit(solution)/shard_map/ppermute | solution.py:19
  41.9 15.4 %collective-permute-start.5 = (f32[256,512]{1,0:T(8,128)}, f32[256,512]{1,0:T(8,128)S(1)}, u32[]{:S(2)}, u32[]{:S(2)}) collective-permute-start(f32[256,512]{1,0:T(8,128)} %collective-permute-done.3), channel_id=1, source_target_pairs={{0,224},{32,0},{64,32},{96,64},{128,96},{160,128},{192,160},{224,1... | collective-permute-start | bytes 1572872 | tf_op jit(solution)/shard_map/ppermute | solution.py:24
  53.5 12.4 %collective-permute-start.6 = (f32[256,512]{1,0:T(8,128)}, f32[256,512]{1,0:T(8,128)S(1)}, u32[]{:S(2)}, u32[]{:S(2)}) collective-permute-start(f32[256,512]{1,0:T(8,128)} %collective-permute-done.4), channel_id=1, source_target_pairs={{0,32},{32,64},{64,96},{96,128},{128,160},{160,192},{192,224},{224... | collective-permute-start | bytes 1572872 | tf_op jit(solution)/shard_map/ppermute | solution.py:19
  73.6 165.3 %all-gather.10.cloned.1.call-start = ((), (), s32[]{:S(2)}) async-start(), calls=%async_computation.4 | async-start | bytes 4718592 | tf_op jit(solution)/shard_map/all_gather | solution.py:154
  80.9 11.5 %copy-start.9 = (s32[1,4]{1,0:T(1,128)S(1)}, s32[1,4]{1,0:T(1,128)}, u32[]{:S(2)}) copy-start(s32[1,4]{1,0:T(1,128)} %param.17) | copy-start | bytes 52
  80.9 67.1 %copy-start.4 = (f32[64,2048]{1,0:T(8,128)S(1)}, f32[64,2048]{1,0:T(8,128)}, u32[]{:S(2)}) copy-start(f32[64,2048]{1,0:T(8,128)} %param.23) | copy-start | bytes 1572868
  82.6 193.3 %all-to-all-start = ((f32[8,256,256]{1,2,0:T(8,128)}), f32[8,256,256]{1,2,0:T(8,128)S(1)}, u32[]{:S(2)}, u32[]{:S(2)}) async-start(f32[8,256,256]{1,2,0:T(8,128)} %broadcast_in_dim.19), calls=%async_computation | async-start | bytes 4194304 | tf_op jit(solution)/shard_map/all_to_all | solution.py:43
  92.2 173.0 %all-gather.14.cloned.1.call-start = ((), (), s32[]{:S(2)}) async-start(), calls=%async_computation.6 | async-start | bytes 1310720 | tf_op jit(solution)/shard_map/all_gather | solution.py:60
  92.6 64.0 %copy-start.10 = (s32[1,4]{1,0:T(1,128)S(1)}, s32[1,4]{1,0:T(1,128)}, u32[]{:S(2)}) copy-start(s32[1,4]{1,0:T(1,128)} %param.18) | copy-start | bytes 52
  156.2 207.1 %all-gather.16.cloned.1.call-start = ((), (), s32[]{:S(2)}) async-start(), calls=%async_computation.7 | async-start | bytes 9437184 | tf_op jit(solution)/shard_map/all_gather | solution.py:60
  275.9 28.4 %all-to-all-start.1 = ((f32[4,1,131078]{2,1,0:T(1,128)}), f32[4,1,131078]{2,1,0:T(1,128)}, u32[]{:S(2)}, u32[]{:S(2)}) async-start(f32[4,1,131078]{2,1,0:T(1,128)} %copy.34), calls=%async_computation.1 | async-start | bytes 4198400 | tf_op jit(solution)/shard_map/all_to_all | solution.py:36
  285.9 31.5 %copy-start.3 = (f32[256,256]{1,0:T(8,128)}, f32[256,256]{1,0:T(8,128)S(1)}, u32[]{:S(2)}) copy-start(f32[256,256]{1,0:T(8,128)S(1)} %fusion.47) | copy-start | bytes 786436
  285.9 27.9 %copy-start.2 = (f32[512,256]{1,0:T(8,128)S(1)}, f32[512,256]{1,0:T(8,128)}, u32[]{:S(2)}) copy-start(f32[512,256]{1,0:T(8,128)} %fusion.9) | copy-start | bytes 1572868
  305.8 34.2 %all-to-all-start.2 = ((f32[8,256,256]{1,2,0:T(8,128)}), f32[8,256,256]{1,2,0:T(8,128)}, u32[]{:S(2)}, u32[]{:S(2)}) async-start(f32[8,256,256]{1,2,0:T(8,128)} %broadcast_in_dim.23), calls=%async_computation.2 | async-start | bytes 4194304 | tf_op jit(solution)/shard_map/all_to_all | solution.py:43
  363.3 11.7 %copy-start.1 = (f32[1,256,2048]{2,1,0:T(8,128)S(1)}, f32[1,256,2048]{2,1,0:T(8,128)}, u32[]{:S(2)}) copy-start(f32[1,256,2048]{2,1,0:T(8,128)} %param.15) | copy-start | bytes 6291460
  (3 other events, 11.5 us)
Sparse Core Ops, SparseCore 0:
  9.8 38.8 all-gather.17
  51.3 96.6 all-gather.7
  150.4 52.4 all-gather.11
  205.1 33.7 all-gather.9
  241.1 24.0 all-gather.13
  266.9 96.3 all-gather.15
